TPU v7x, 32 devices: a whole 2x2x4 slice. The times are simulated.
32 devices in a mesh: tensor: 4 (over z), dp: 8 (over y, x, core).
Axes of the slice: x: 2, y: 2, z: 4, core: 2. Of those that a mesh axis runs over, the one named last changes fastest.
Arguments:
- grads: bfloat16 [8, 40, 28672], P('dp', None, 'tensor'), may hold values from -6 to 6
- offload_mask: int32 [8, 5], replicated, may hold values from 0 to 1, as said below
- owner_map: int32 [8], replicated, may hold values from 0 to 7, as said below
- local_master: float32 [24, 28672], P('dp', 'tensor'), may hold values from -6 to 6
- local_moment: float32 [24, 28672], P('dp', 'tensor'), may hold values from -1.2 to 1.2
- local_second: float32 [24, 28672], P('dp', 'tensor'), may hold values from 0.001 to 0.1
- offload_master: float32 [16, 2, 28672], P('dp', None, 'tensor'), may hold values from -6 to 6
- offload_moment: float32 [16, 2, 28672], P('dp', None, 'tensor'), may hold values from -1.2 to 1.2
- offload_second: float32 [16, 2, 28672], P('dp', None, 'tensor'), may hold values from 0.001 to 0.1
Outputs:
- new_weights: bfloat16 [40, 28672], P(None, 'tensor')
- grad_norm: float32 [], replicated
- new_local_master: float32 [24, 28672], P('dp', 'tensor')
- new_local_moment: float32 [24, 28672], P('dp', 'tensor')
- new_local_second: float32 [24, 28672], P('dp', 'tensor')
- new_offload_master: float32 [16, 2, 28672], P('dp', None, 'tensor')
- new_offload_moment: float32 [16, 2, 28672], P('dp', None, 'tensor')
- new_offload_second: float32 [16, 2, 28672], P('dp', None, 'tensor')
Inputs may be any that keep to these rules, and one draw needn't show every extreme that they name: Each row of offload_mask holds exactly 2 ones. `owner_map`: no device is named by more than 2 shards, and some device is named by exactly 2.
All inputs are finite; a program needn't handle non-finite values.
Results may differ from a plain program's by a relative error of at most 0.0039.
Values may be sent and summed in bfloat16 or wider, within the bound.
A program may use at most 128 MiB of HBM per device.

v0:
```python
import jax
import jax.numpy as jnp
from jax import lax
from jax.sharding import PartitionSpec as P

beta_first = 0.9
beta_second = 0.95
learn_rate = 0.02
decay_rate = 0.1
epsilon_value = 1e-08
step_count = 10
bias_first = 1.0 - beta_first**step_count
bias_second = 1.0 - beta_second**step_count


def adam_update(master, moment, second, gradient):
    moment_new = beta_first * moment + (1.0 - beta_first) * gradient
    second_new = beta_second * second + (1.0 - beta_second) * gradient * gradient
    scaled = moment_new / bias_first / (jnp.sqrt(second_new / bias_second) + epsilon_value)
    master_new = master - learn_rate * (scaled + decay_rate * master)
    return (master_new, moment_new, second_new)


def row_tables(offload_mask, owner_map):
    shards = owner_map.shape[0]
    row_dev = offload_mask.shape[1]
    numbers = jnp.arange(shards, dtype=jnp.int32)
    same_owner = owner_map[:, None] == owner_map[None, :]
    earlier = numbers[None, :] < numbers[:, None]
    slot_of = jnp.sum((same_owner & earlier).astype(jnp.int32), axis=1)
    off_rank = jnp.cumsum(offload_mask, axis=1) - offload_mask
    keep_rank = jnp.arange(row_dev, dtype=jnp.int32)[None, :] - off_rank
    return (slot_of, off_rank, keep_rank)


def body(
    grads,
    offload_mask,
    owner_map,
    local_master,
    local_moment,
    local_second,
    offload_master,
    offload_moment,
    offload_second,
):
    devices = lax.axis_size("dp")
    position = lax.axis_index("dp")
    row_dev = offload_mask.shape[1]
    kept_count = local_master.shape[0]
    slot_count = offload_master.shape[0]
    offloaded = offload_master.shape[1]
    columns = grads.shape[2]
    slot_of, off_rank, keep_rank = row_tables(offload_mask, owner_map)
    is_off = offload_mask == 1
    row_range = jnp.arange(row_dev, dtype=jnp.int32)[None, None, :]
    off_hits = is_off[:, None, :] & (
        off_rank[:, None, :] == jnp.arange(offloaded, dtype=jnp.int32)[None, :, None]
    )
    off_index = jnp.sum(jnp.where(off_hits, row_range, 0), axis=2)
    keep_hits = ~is_off[:, None, :] & (
        keep_rank[:, None, :] == jnp.arange(kept_count, dtype=jnp.int32)[None, :, None]
    )
    keep_index = jnp.sum(jnp.where(keep_hits, row_range, 0), axis=2)
    shard_numbers = jnp.arange(devices, dtype=jnp.int32)
    matches = (owner_map[None, None, :] == shard_numbers[:, None, None]) & (
        slot_of[None, None, :] == jnp.arange(slot_count, dtype=jnp.int32)[None, :, None]
    )
    source_of = jnp.sum(jnp.where(matches, shard_numbers[None, None, :], 0), axis=2)
    filled = jnp.any(matches, axis=2)
    my_filled = jnp.take(filled, position, axis=0)
    local_grads = grads[0]
    keep_rows = shard_numbers[:, None] * row_dev + keep_index
    slot_rows = source_of[:, :, None] * row_dev + jnp.take(off_index, source_of, axis=0)
    row_table = jnp.concatenate(
        [keep_rows, slot_rows.reshape(devices, slot_count * offloaded)], axis=1
    ).reshape(-1)
    row_weights = jnp.concatenate(
        [
            jnp.ones((devices, kept_count), jnp.float32),
            jnp.repeat(filled.astype(jnp.float32), offloaded, axis=1),
        ],
        axis=1,
    ).reshape(-1)
    my_grads = (
        lax.psum_scatter(
            jnp.take(local_grads, row_table, axis=0).astype(jnp.float32) * row_weights[:, None],
            "dp",
            scatter_dimension=0,
            tiled=True,
        )
        / devices
    )
    keep_grad = my_grads[:kept_count]
    slot_grad = my_grads[kept_count:].reshape(slot_count, offloaded, columns)
    partial_value = jnp.sum(my_grads * my_grads)
    grad_norm = jnp.sqrt(lax.psum(partial_value, ("tensor", "dp")))
    new_local = adam_update(local_master, local_moment, local_second, keep_grad)
    updated = adam_update(offload_master, offload_moment, offload_second, slot_grad)
    formers = (offload_master, offload_moment, offload_second)
    slot_mask = my_filled[:, None, None]
    new_off = tuple((jnp.where(slot_mask, updated[place], formers[place]) for place in range(3)))
    keep_bf = new_local[0].astype(jnp.bfloat16)
    slot_bf = new_off[0].astype(jnp.bfloat16)
    back_out = jnp.where(
        (owner_map == position)[:, None, None],
        jnp.take(slot_bf, slot_of, axis=0),
        jnp.zeros((), jnp.bfloat16),
    )
    back_in = lax.all_to_all(back_out, "dp", split_axis=0, concat_axis=0, tiled=True)
    mine_off = jnp.take(back_in, jnp.take(owner_map, position), axis=0)
    stacked = jnp.concatenate([keep_bf, mine_off], axis=0)
    order_rows = jnp.where(
        jnp.take(is_off, position, axis=0),
        kept_count + jnp.take(off_rank, position, axis=0),
        jnp.take(keep_rank, position, axis=0),
    )
    new_weights = lax.all_gather(jnp.take(stacked, order_rows, axis=0), "dp", axis=0, tiled=True)
    return (
        new_weights,
        grad_norm,
        new_local[0],
        new_local[1],
        new_local[2],
        new_off[0],
        new_off[1],
        new_off[2],
    )


def solution(mesh):
    return jax.shard_map(
        body,
        mesh=mesh,
        in_specs=(
            P("dp", None, "tensor"),
            P(),
            P(),
            P("dp", "tensor"),
            P("dp", "tensor"),
            P("dp", "tensor"),
            P("dp", None, "tensor"),
            P("dp", None, "tensor"),
            P("dp", None, "tensor"),
        ),
        out_specs=(
            P(None, "tensor"),
            P(),
            P("dp", "tensor"),
            P("dp", "tensor"),
            P("dp", "tensor"),
            P("dp", None, "tensor"),
            P("dp", None, "tensor"),
            P("dp", None, "tensor"),
        ),
        check_vma=False,
    )
```

profile of v0, /device:TPU:0, one launch (start us, length us, event | category | flops | bytes accessed | tf_op | source)
XLA Modules:
  0.0 106.5 jit_solution(14819365956823482855)
XLA Ops:
  0.6 0.0 copy-start
  0.6 0.9 convert_reduce_fusion
  1.6 0.7 iota_compare_fusion.2
  2.2 0.1 fusion.5
  2.4 0.1 copy.50
  2.5 0.1 reshape.334
  2.6 0.7 fusion.16
  3.3 0.8 reduce_window_sum.11
  4.1 0.7 iota_subtract_fusion
  4.8 0.1 copy.49
  4.9 0.1 copy.48
  5.0 0.1 copy.51
  5.1 0.6 gather_fusion
  5.7 0.1 copy.57
  5.8 0.1 copy.46
  5.9 0.1 copy.47
  6.0 0.1 copy.53
  6.1 0.1 copy.45
  6.2 0.1 copy.44
  6.3 0.1 copy.54
  6.4 0.1 reshape.180
  6.5 0.1 reshape.179
  6.5 0.1 and_reduce_fusion
  6.8 0.1 copy.58
  6.8 0.1 concatenate.10.clone
  6.9 0.1 mul.99
  7.0 0.0 copy-done
  7.0 1.1 gather_fusion.1
  8.1 0.2 convert_multiply_fusion
  8.3 0.0 copy-start.7
  8.3 0.0 copy-start.8
  8.3 26.0 %fusion = f32[8,7168]{1,0:T(8,128)S(1)} fusion(f32[56,7168]{1,0:T(8,128)S(1)} %convert_multiply_fusion), kind=kCustom, calls=%all-reduce-scatter | all-reduce-scatter fusion | flops 458753 | bytes 1835520
  34.3 0.0 copy-start.1
  34.4 0.0 copy-start.2
  34.4 0.0 copy-start.3
  34.4 1.4 %collective-permute-start = (f32[7,7168]{1,0:T(8,128)S(1)}, f32[7,7168]{1,0:T(8,128)S(1)}, u32[]{:S(2)}, u32[]{:S(2)}) collective-permute-start(f32[7,7168]{1,0:T(8,128)S(1)} %slice.53), channel_id=1, source_target_pairs={{0,1},{1,2},{2,3},{3,4},{4,5},{5,6},{6,7},{8,9},{9,10},{10,11},{11... | collective-permute-start | bytes 602120
  35.9 0.0 copy-done.7
  35.9 0.6 dynamic-slice.16
  36.5 0.2 select_reduce_fusion.1
  37.4 0.0 copy-done.8
  37.4 0.6 dynamic-slice.26
  38.6 0.0 collective-permute-done
  38.7 0.4 concatenate.17
  39.0 0.0 copy-start.4
  39.0 0.0 copy-start.5
  39.0 0.0 copy-start.6
  39.1 0.7 multiply_reduce_fusion
  39.8 0.1 reshape.182
  39.9 0.0 copy-done.1
  39.9 0.0 copy-done.2
  39.9 0.0 copy-done.3
  39.9 1.2 %fusion.15 = (bf16[2,2,7168]{2,1,0:T(2,128)(2,1)S(1)}, f32[2,2,7168]{2,1,0:T(2,128)}, f32[2,2,7168]{2,1,0:T(2,128)}, f32[2,2,7168]{2,1,0:T(2,128)}) fusion(f32[2,2,7168]{2,1,0:T(2,128)S(1)} %copy-done.1, f32[2,2,7168]{2,1,0:T(2,128)S(1)} %reshape.182, f32[2,2,7168]{2,1,0:T(2,128)S(1)} %copy-done.2, f32[2,2,7168]{2,1,0:T(2,128)S(1)} %copy-done.3, ...), kind=kLoop, calls=%fused_computation.71 | loop fusion | flops 544768 | bytes 860162 | tf_op jit(solution)/shard_map/convert_element_type | solution.py:104
  41.1 1.0 gather_fusion.2
  42.1 1.0 broadcast_select_fusion.1
  43.1 6.1 %all-to-all-start = ((bf16[8,2,7168]{2,1,0:T(2,128)(2,1)}), bf16[8,2,7168]{2,1,0:T(2,128)(2,1)S(1)}, u32[]{:S(2)}, u32[]{:S(2)}) async-start(bf16[8,2,7168]{2,1,0:T(2,128)(2,1)} %broadcast_select_fusion.1), calls=%async_computation | async-start | bytes 458752 | tf_op jit(solution)/shard_map/all_to_all | solution.py:110
  49.2 0.0 copy-done.4
  49.2 0.9 fusion.13
  50.1 41.1 %psum.7 = f32[]{:T(128)} all-reduce(f32[]{:T(128)} %get-tuple-element.64), channel_id=1, replica_groups=mesh['tensor'=4,'dp'=8] {'tensor','dp'}, use_global_device_ids=true, to_apply=%region_8.10 | all-reduce | flops 1 | bytes 8 | tf_op jit(solution)/shard_map/psum | solution.py:97
  91.9 0.0 all-to-all-done
  91.9 0.1 pad_maximum_fusion
  92.0 0.6 gather_fusion.3
  92.6 0.1 select_bitcast_fusion
  92.7 11.6 %all-gather = bf16[8,5,7168]{2,1,0:T(8,128)(2,1)S(1)} all-gather(bf16[1,5,7168]{2,1,0:T(8,128)(2,1)S(1)} %select_bitcast_fusion), channel_id=1, replica_groups=mesh['tensor'=4,'dp'=8] {'dp'}, dimensions={0}, use_global_device_ids=true | all-gather | bytes 645120 | tf_op jit(solution)/shard_map/all_gather | solution.py:118
  104.3 1.1 %reshape.367 = bf16[40,7168]{1,0:T(8,128)(2,1)} reshape(bf16[8,5,7168]{2,1,0:T(8,128)(2,1)S(1)} %all-gather) | data formatting | bytes 1146880
  (26 shorter events, 0.3 us)
Async XLA Ops:
  0.6 6.4 %copy-start = (bf16[1,40,7168]{2,1,0:T(8,128)(2,1)S(1)}, bf16[1,40,7168]{2,1,0:T(8,128)(2,1)}, u32[]{:S(2)}) copy-start(bf16[1,40,7168]{2,1,0:T(8,128)(2,1)} %param.11) | copy-start | bytes 1720324
  8.3 27.6 %copy-start.7 = (s32[8]{0:T(128)S(1)}, s32[8]{0:T(128)}, u32[]{:S(2)}) copy-start(s32[8]{0:T(128)} %param.13) | copy-start | bytes 100
  8.3 29.1 %copy-start.8 = (u32[32]{0:T(128)S(1)}, u32[32]{0:T(128)}, u32[]{:S(2)}) copy-start(u32[32]{0:T(128)} %constant.288) | copy-start | bytes 388
  34.3 5.5 %copy-start.1 = (f32[2,2,7168]{2,1,0:T(2,128)S(1)}, f32[2,2,7168]{2,1,0:T(2,128)}, u32[]{:S(2)}) copy-start(f32[2,2,7168]{2,1,0:T(2,128)} %param.17) | copy-start | bytes 344068
  34.4 5.5 %copy-start.2 = (f32[2,2,7168]{2,1,0:T(2,128)S(1)}, f32[2,2,7168]{2,1,0:T(2,128)}, u32[]{:S(2)}) copy-start(f32[2,2,7168]{2,1,0:T(2,128)} %param.19) | copy-start | bytes 344068
  34.4 5.5 %copy-start.3 = (f32[2,2,7168]{2,1,0:T(2,128)S(1)}, f32[2,2,7168]{2,1,0:T(2,128)}, u32[]{:S(2)}) copy-start(f32[2,2,7168]{2,1,0:T(2,128)} %param.18) | copy-start | bytes 344068
  34.4 4.2 %collective-permute-start = (f32[7,7168]{1,0:T(8,128)S(1)}, f32[7,7168]{1,0:T(8,128)S(1)}, u32[]{:S(2)}, u32[]{:S(2)}) collective-permute-start(f32[7,7168]{1,0:T(8,128)S(1)} %slice.53), channel_id=1, source_target_pairs={{0,1},{1,2},{2,3},{3,4},{4,5},{5,6},{6,7},{8,9},{9,10},{10,11},{11... | collective-permute-start | bytes 602120
  39.0 10.2 %copy-start.4 = (f32[3,7168]{1,0:T(4,128)S(1)}, f32[3,7168]{1,0:T(4,128)}, u32[]{:S(2)}) copy-start(f32[3,7168]{1,0:T(4,128)} %param.14) | copy-start | bytes 258052
  39.0 10.2 %copy-start.5 = (f32[3,7168]{1,0:T(4,128)S(1)}, f32[3,7168]{1,0:T(4,128)}, u32[]{:S(2)}) copy-start(f32[3,7168]{1,0:T(4,128)} %param.15) | copy-start | bytes 258052
  39.0 10.2 %copy-start.6 = (f32[3,7168]{1,0:T(4,128)S(1)}, f32[3,7168]{1,0:T(4,128)}, u32[]{:S(2)}) copy-start(f32[3,7168]{1,0:T(4,128)} %param.16) | copy-start | bytes 258052
  43.1 48.8 %all-to-all-start = ((bf16[8,2,7168]{2,1,0:T(2,128)(2,1)}), bf16[8,2,7168]{2,1,0:T(2,128)(2,1)S(1)}, u32[]{:S(2)}, u32[]{:S(2)}) async-start(bf16[8,2,7168]{2,1,0:T(2,128)(2,1)} %broadcast_select_fusion.1), calls=%async_computation | async-start | bytes 458752 | tf_op jit(solution)/shard_map/all_to_all | solution.py:110
where the time goes:
time: 107 us
  blocking collectives  78.7 us (74%)
  other arithmetic  8.58 us (8%)
  starting transfers between devices  7.55 us (7%)
  local copies, waits for them, and re-layouts  7.5 us (7%)
  between operations  4.15 us (4%)
    psum x1, blocking collectives, body(): grad_norm = jnp.sqrt(lax.psum(partial_value, ('tensor', 'dp')))  41.1 us
    unnamed x1, blocking collectives  26 us
    all_gather x1, blocking collectives, body(): lax.all_gather(jnp.take(stacked, order_rows, axis=0), 'dp', axis=0, tiled...  11.6 us
    all_to_all x1, starting transfers between devices, body(): lax.all_to_all(back_out, 'dp', split_axis=0, concat_axis=0, tiled=True)  6.12 us
    unnamed x23, local copies, waits for them, and re-layouts  2.18 us
  transfers between devices with their start and end apart: 2, of which 0 were waited for; matrix products, arithmetic and copies ran while one was open for 2% of the time, Pallas kernels for 0%

commit v1 on v0

v1 whole, which is shorter than its diff:
```python
import functools

import jax
import jax.numpy as jnp
from jax import lax
from jax.experimental import pallas as pl
from jax.experimental.pallas import tpu as pltpu
from jax.sharding import PartitionSpec as P

MESH = pl.DeviceIdType.MESH
beta_first = 0.9
beta_second = 0.95
learn_rate = 0.02
decay_rate = 0.1
epsilon_value = 1e-08
step_count = 10
bias_first = 1.0 - beta_first**step_count
bias_second = 1.0 - beta_second**step_count
LANES = 128
SUBLANES = 8


def adam_update(master, moment, second, gradient):
    moment_new = beta_first * moment + (1.0 - beta_first) * gradient
    second_new = beta_second * second + (1.0 - beta_second) * gradient * gradient
    scaled = moment_new / bias_first / (jnp.sqrt(second_new / bias_second) + epsilon_value)
    master_new = master - learn_rate * (scaled + decay_rate * master)
    return (master_new, moment_new, second_new)


def kernel(
    n,
    tensors,
    chunks,
    mask_ref,
    owner_ref,
    grads,
    lm_in,
    l1_in,
    l2_in,
    om_in,
    o1_in,
    o2_in,
    out_w,
    out_norm,
    lm_out,
    l1_out,
    l2_out,
    om_out,
    o1_out,
    o2_out,
    mine,
    other,
    sendbuf,
    recvbuf,
    wall,
    w32,
    obuf,
    lst,
    ost,
    tsum,
    dsum,
    tpart,
    dpart,
    load_sem,
    state_sem,
    store_sem,
    pair_s,
    pair_r,
    rs_s,
    rs_r,
    ag_s,
    ag_r,
    fw_s,
    fw_r,
    t_s,
    t_r,
    d_s,
    d_r,
):
    dp = lax.axis_index("dp")
    tn = lax.axis_index("tensor")
    core = lax.rem(dp, 2)
    chip = dp // 2
    chips = n // 2
    partner = chip * 2 + 1 - core
    rows, columns = mine.shape
    row_dev = rows // n
    kept = lst.shape[1]
    slots, off = ost.shape[1], ost.shape[2]
    width = columns // chunks
    pad = w32.shape[0]

    load = pltpu.make_async_copy(grads.at[0], mine, load_sem)
    load.start()
    loads = []
    for i, (ref, dst) in enumerate(
        zip((lm_in, l1_in, l2_in, om_in, o1_in, o2_in), [lst.at[i] for i in range(3)] + [ost.at[i] for i in range(3)])
    ):
        cp = pltpu.make_async_copy(ref, dst, state_sem.at[i])
        cp.start()
        loads.append(cp)

    barrier = pltpu.get_barrier_semaphore()

    def greet(k, c):
        pl.semaphore_signal(barrier, inc=1, device_id={"dp": lax.rem(dp + k, n)}, device_id_type=MESH)
        return c

    lax.fori_loop(1, n, greet, 0)
    for k in range(1, tensors):
        pl.semaphore_signal(barrier, inc=1, device_id={"tensor": lax.rem(tn + k, tensors)}, device_id_type=MESH)

    lane = lax.broadcasted_iota(jnp.int32, (1, rows), 1)
    sub = lax.broadcasted_iota(jnp.int32, (rows, 1), 0)

    def shard(s, carry):
        by_lane, by_sub, count = carry
        owner = owner_ref[s]
        count = count + jnp.where(owner == dp, 1, 0)

        def earlier(e, slot):
            return slot + jnp.where((owner_ref[e] == owner) & (e < s), 1, 0)

        slot = lax.fori_loop(0, n, earlier, 0)
        rank = jnp.int32(0)
        for j in range(row_dev):
            m = mask_ref[s, j]
            target = jnp.where(m == 1, owner * pad + kept + slot * off + rank, s * pad + (j - rank))
            rank = rank + m
            by_lane = jnp.where(lane == s * row_dev + j, target, by_lane)
            by_sub = jnp.where(sub == s * row_dev + j, target, by_sub)
        return by_lane, by_sub, count

    by_lane, by_sub, count = lax.fori_loop(
        0, n, shard, (jnp.zeros((1, rows), jnp.int32), jnp.zeros((rows, 1), jnp.int32), jnp.int32(0))
    )
    place = lax.broadcasted_iota(jnp.int32, (chips * pad, rows), 0)
    goal = (place // pad * 2 + core) * pad + place % pad
    route = jnp.where(goal == by_lane, 1.0, 0.0).astype(jnp.bfloat16)
    back = jnp.where(lax.broadcasted_iota(jnp.int32, (rows, n * pad), 1) == by_sub, 1.0, 0.0).astype(jnp.bfloat16)

    load.wait()
    pl.semaphore_wait(barrier, n - 1 + tensors - 1)

    pairs = []
    for c in range(chunks):
        cols = pl.ds(c * width, width)
        cp = pltpu.make_async_remote_copy(
            mine.at[:, cols], other.at[:, cols], pair_s.at[c], pair_r.at[c], device_id={"dp": partner}, device_id_type=MESH
        )
        cp.start()
        pairs.append(cp)

    scatter = []
    for c in range(chunks):
        cols = pl.ds(c * width, width)
        pairs[c].wait_recv()
        both = mine[:, cols].astype(jnp.float32) + other[:, cols].astype(jnp.float32)
        routed = jnp.dot(route, both.astype(jnp.bfloat16), preferred_element_type=jnp.float32)
        sendbuf[:, :, cols] = routed.reshape(chips, pad, width).astype(jnp.bfloat16)
        row = []
        for k in range(1, chips):
            to = lax.rem(chip + k, chips)
            cp = pltpu.make_async_remote_copy(
                sendbuf.at[to, :, cols],
                recvbuf.at[k - 1, :, cols],
                rs_s.at[k - 1, c],
                rs_r.at[k - 1, c],
                device_id={"dp": to * 2 + core},
                device_id_type=MESH,
            )
            cp.start()
            row.append(cp)
        scatter.append(row)

    for cp in loads:
        cp.wait()
    w32[...] = jnp.zeros_like(w32)
    squares = jnp.zeros((pad, LANES), jnp.float32)
    gather, own, stores = [], [], []
    for c in range(chunks):
        cols = pl.ds(c * width, width)
        total = sendbuf[chip, :, cols].astype(jnp.float32)
        for k in range(1, chips):
            scatter[c][k - 1].wait_recv()
            total = total + recvbuf[k - 1, :, cols].astype(jnp.float32)
        total = total / n
        sq = total * total
        for v in range(width // LANES):
            squares = squares + sq[:, v * LANES : (v + 1) * LANES]
        new = adam_update(lst[0, :, cols], lst[1, :, cols], lst[2, :, cols], total[:kept])
        for i in range(3):
            lst[i, :, cols] = new[i]
        w32[:kept, cols] = new[0]
        for s in range(slots):
            first = kept + s * off
            old = (ost[0, s, :, cols], ost[1, s, :, cols], ost[2, s, :, cols])
            new = adam_update(*old, total[first : first + off])
            filled = jnp.full(old[0].shape, count, jnp.int32) > s
            for i in range(3):
                value = jnp.where(filled, new[i], old[i])
                ost[i, s, :, cols] = value
                if i == 0:
                    w32[first : first + off, cols] = value
        wall[dp, :, cols] = w32[:, cols].astype(jnp.bfloat16)
        row = []
        for k in range(1, chips):
            to = lax.rem(chip + k, chips)
            cp = pltpu.make_async_remote_copy(
                wall.at[dp, :, cols],
                wall.at[dp, :, cols],
                ag_s.at[k - 1, c],
                ag_r.at[k - 1, c],
                device_id={"dp": to * 2 + core},
                device_id_type=MESH,
            )
            cp.start()
            row.append(cp)
        gather.append(row)
        cp = pltpu.make_async_remote_copy(
            wall.at[dp, :, cols],
            wall.at[dp, :, cols],
            fw_s.at[0, c],
            fw_r.at[0, c],
            device_id={"dp": partner},
            device_id_type=MESH,
        )
        cp.start()
        own.append(cp)

    for i, (ref, src) in enumerate(
        zip((lm_out, l1_out, l2_out, om_out, o1_out, o2_out), [lst.at[i] for i in range(3)] + [ost.at[i] for i in range(3)])
    ):
        cp = pltpu.make_async_copy(src, ref, state_sem.at[i])
        cp.start()
        stores.append(cp)

    tpart[...] = squares
    tcopies = []
    for k in range(1, tensors):
        cp = pltpu.make_async_remote_copy(
            tpart, tsum.at[k - 1], t_s.at[k - 1], t_r.at[k - 1], device_id={"tensor": lax.rem(tn + k, tensors)}, device_id_type=MESH
        )
        cp.start()
        tcopies.append(cp)
    for cp in tcopies:
        cp.wait()

    value = tpart[...]
    for k in range(1, tensors):
        value = value + tsum[k - 1]
    dpart[...] = value
    dcopies = []
    for k in range(1, n):
        cp = pltpu.make_async_remote_copy(
            dpart, dsum.at[k - 1], d_s.at[k - 1], d_r.at[k - 1], device_id={"dp": lax.rem(dp + k, n)}, device_id_type=MESH
        )
        cp.start()
        dcopies.append(cp)

    forwards = []
    for c in range(chunks):
        cols = pl.ds(c * width, width)
        row = [own[c]]
        for k in range(1, chips):
            gather[c][k - 1].wait_recv()
            src = lax.rem(chip + chips - k, chips) * 2 + core
            cp = pltpu.make_async_remote_copy(
                wall.at[src, :, cols],
                wall.at[src, :, cols],
                fw_s.at[k, c],
                fw_r.at[k, c],
                device_id={"dp": partner},
                device_id_type=MESH,
            )
            cp.start()
            row.append(cp)
        forwards.append(row)

    outs = []
    for c in range(chunks):
        cols = pl.ds(c * width, width)
        for cp in forwards[c]:
            cp.wait_recv()
        weights = wall[:, :, cols].reshape(n * pad, width)
        obuf[:, cols] = jnp.dot(back, weights, preferred_element_type=jnp.float32).astype(jnp.bfloat16)
        cp = pltpu.make_async_copy(obuf.at[:, cols], out_w.at[:, cols], store_sem.at[c])
        cp.start()
        outs.append(cp)

    value = dpart[...]
    for k in range(1, n):
        dcopies[k - 1].wait()
        value = value + dsum[k - 1]
    out_norm[...] = jnp.sqrt(jnp.sum(value, keepdims=True))

    for c in range(chunks):
        pairs[c].wait_send()
        for k in range(1, chips):
            scatter[c][k - 1].wait_send()
            gather[c][k - 1].wait_send()
        for cp in forwards[c]:
            cp.wait_send()
    for cp in stores:
        cp.wait()
    for cp in outs:
        cp.wait()


def body(n, tensors, grads, mask, owner, *states):
    rows, columns = grads.shape[1:]
    local, offload = states[0], states[3]
    chunks = 4
    while columns % (chunks * LANES):
        chunks -= 1
    chips = n // 2
    used = local.shape[0] + offload.shape[0] * offload.shape[1]
    pad = -(-used // SUBLANES) * SUBLANES
    any_space = pl.BlockSpec(memory_space=pl.ANY)
    smem = pl.BlockSpec(memory_space=pltpu.SMEM)
    dma = pltpu.SemaphoreType.DMA
    f32, bf16 = jnp.float32, jnp.bfloat16
    outs = pl.pallas_call(
        functools.partial(kernel, n, tensors, chunks),
        out_shape=[jax.ShapeDtypeStruct((rows, columns), bf16), jax.ShapeDtypeStruct((1, 1), f32)]
        + [jax.ShapeDtypeStruct(s.shape, f32) for s in states],
        in_specs=[smem, smem] + [any_space] * 7,
        out_specs=[any_space, pl.BlockSpec(memory_space=pltpu.VMEM)] + [any_space] * 6,
        scratch_shapes=[
            pltpu.VMEM((rows, columns), bf16),
            pltpu.VMEM((rows, columns), bf16),
            pltpu.VMEM((chips, pad, columns), bf16),
            pltpu.VMEM((chips - 1, pad, columns), bf16),
            pltpu.VMEM((n, pad, columns), bf16),
            pltpu.VMEM((pad, columns), f32),
            pltpu.VMEM((rows, columns), bf16),
            pltpu.VMEM((3,) + local.shape, f32),
            pltpu.VMEM((3,) + offload.shape, f32),
            pltpu.VMEM((tensors - 1, pad, LANES), f32),
            pltpu.VMEM((n - 1, pad, LANES), f32),
            pltpu.VMEM((pad, LANES), f32),
            pltpu.VMEM((pad, LANES), f32),
            dma,
            dma((6,)),
            dma((chunks,)),
            dma((chunks,)),
            dma((chunks,)),
            dma((chips - 1, chunks)),
            dma((chips - 1, chunks)),
            dma((chips - 1, chunks)),
            dma((chips - 1, chunks)),
            dma((chips, chunks)),
            dma((chips, chunks)),
            dma((tensors - 1,)),
            dma((tensors - 1,)),
            dma((n - 1,)),
            dma((n - 1,)),
        ],
        compiler_params=pltpu.CompilerParams(collective_id=0, has_side_effects=True),
        name="step",
    )(mask, owner, grads, *states)
    return (outs[0], outs[1][0, 0]) + tuple(outs[2:])


def solution(mesh):
    local, offload = P("dp", "tensor"), P("dp", None, "tensor")
    return jax.shard_map(
        functools.partial(body, mesh.shape["dp"], mesh.shape["tensor"]),
        mesh=mesh,
        in_specs=(P("dp", None, "tensor"), P(), P()) + (local,) * 3 + (offload,) * 3,
        out_specs=(P(None, "tensor"), P()) + (local,) * 3 + (offload,) * 3,
        check_vma=False,
    )
```

time: 107 us -> 34 us (0.32)
  blocking collectives: 78.7 us -> 0 us
  Pallas kernels: 0 us -> 24 us
  other arithmetic: 8.58 us -> 0 us
  starting transfers between devices: 7.55 us -> 0 us
  between operations: 4.15 us -> 2.44 us
    psum x1 -> x0, blocking collectives: 41.1 us -> none  [body(): grad_norm = jnp.sqrt(lax.psum(partial_value, ('tensor', 'dp')))]
    unnamed x1 -> x0, blocking collectives: 26 us -> none
    pallas_call x0 -> x1, Pallas kernels: none -> 24 us  [body(): pl.pallas_call(functools.partial(kernel, n, tensors, chunks), out_shape=[...]
    all_gather x1 -> x0, blocking collectives: 11.6 us -> none  [body(): lax.all_gather(jnp.take(stacked, order_rows, axis=0), 'dp', axis=0, tiled...]
    all_to_all x1 -> x0, starting transfers between devices: 6.12 us -> none  [body(): lax.all_to_all(back_out, 'dp', split_axis=0, concat_axis=0, tiled=True)]
    unnamed x23 -> x19, local copies, waits for them, and re-layouts: 2.18 us -> 7.28 us
    gather x5 -> x0, local copies, waits for them, and re-layouts: 3.35 us -> none  [the longest x1 1.05 us: body(): jnp.take(local_grads, row_table, axis=0).astype(jnp.float32)]
    convert_element_type x3 -> x0, other arithmetic: 2.07 us -> none  [the longest x1 1.17 us: body(): slot_bf = new_off[0].astype(jnp.bfloat16)]
  transfers between devices with their start and end apart: 2 -> 0, of which waited for: 0 -> 0; matrix products, arithmetic and copies ran while one was open for 2% -> 0% of each run, Pallas kernels for 0% -> 0%
where the time goes in v1:
time: 34 us; the launch traced here: 33.7 us
  Pallas kernels  24 us (71%)
  local copies, waits for them, and re-layouts  7.28 us (21%)
  between operations  2.44 us (7%)
    pallas_call x1, Pallas kernels, body(): pl.pallas_call(functools.partial(kernel, n, tensors, chunks), out_shape=[...  24 us
    unnamed x19, local copies, waits for them, and re-layouts  7.28 us

profile of v1, /device:TPU:0, one launch (start us, length us, event | category | flops | bytes accessed | tf_op | source)
XLA Modules:
  0.0 33.7 jit_solution(316724704439787553)
XLA Ops:
  0.6 24.0 %step.1 = (bf16[40,7168]{1,0:T(8,128)(2,1)}, f32[1,1]{1,0:T(1,128)}, f32[3,7168]{1,0:T(4,128)}, f32[3,7168]{1,0:T(4,128)}, f32[3,7168]{1,0:T(4,128)}, /*index=5*...) custom-call(s32[8,5]{1,0:T(8,128)} %mask_ref.1, s32[8]{0:T(128)} %owner_ref.1, ...), custom_call_target="tpu_custom_call" | custom-call | tf_op jit(solution)/shard_map/step/pallas_call | solution.py:324
  24.6 0.0 copy-start.5
  24.6 1.9 %copy.25 = bf16[40,7168]{1,0:T(8,128)(2,1)} copy(bf16[40,7168]{1,0:T(8,128)(2,1)} %get-tuple-element.32) | data formatting | bytes 1146880
  27.2 0.0 copy-done.5
  27.2 0.0 copy-start.4
  27.2 0.6 %copy.27 = f32[3,7168]{1,0:T(4,128)} copy(f32[3,7168]{1,0:T(4,128)S(1)} %copy-done.5) | data formatting | bytes 172032
  27.9 0.3 copy-done.4
  28.1 0.0 copy-start.3
  28.1 0.6 %copy.28 = f32[3,7168]{1,0:T(4,128)} copy(f32[3,7168]{1,0:T(4,128)S(1)} %copy-done.4) | data formatting | bytes 172032
  28.8 0.3 copy-done.3
  29.1 0.0 copy-start.2
  29.1 0.6 %copy.29 = f32[3,7168]{1,0:T(4,128)} copy(f32[3,7168]{1,0:T(4,128)S(1)} %copy-done.3) | data formatting | bytes 172032
  29.7 0.3 copy-done.2
  30.0 0.0 copy-start.1
  30.0 0.6 %copy.30 = f32[2,2,7168]{2,1,0:T(2,128)} copy(f32[2,2,7168]{2,1,0:T(2,128)S(1)} %copy-done.2) | data formatting | bytes 229376
  30.7 0.3 copy-done.1
  31.0 0.0 copy-start
  31.0 0.6 %copy.31 = f32[2,2,7168]{2,1,0:T(2,128)} copy(f32[2,2,7168]{2,1,0:T(2,128)S(1)} %copy-done.1) | data formatting | bytes 229376
  31.6 0.3 copy-done
  31.9 0.6 %copy.32 = f32[2,2,7168]{2,1,0:T(2,128)} copy(f32[2,2,7168]{2,1,0:T(2,128)S(1)} %copy-done) | data formatting | bytes 229376
Async XLA Ops:
  24.6 2.6 %copy-start.5 = (f32[3,7168]{1,0:T(4,128)S(1)}, f32[3,7168]{1,0:T(4,128)}, u32[]{:S(2)}) copy-start(f32[3,7168]{1,0:T(4,128)} %get-tuple-element.34) | copy-start | bytes 258052
  27.2 0.9 %copy-start.4 = (f32[3,7168]{1,0:T(4,128)S(1)}, f32[3,7168]{1,0:T(4,128)}, u32[]{:S(2)}) copy-start(f32[3,7168]{1,0:T(4,128)} %get-tuple-element.35) | copy-start | bytes 258052
  28.1 0.9 %copy-start.3 = (f32[3,7168]{1,0:T(4,128)S(1)}, f32[3,7168]{1,0:T(4,128)}, u32[]{:S(2)}) copy-start(f32[3,7168]{1,0:T(4,128)} %get-tuple-element.36) | copy-start | bytes 258052
  29.1 0.9 %copy-start.2 = (f32[2,2,7168]{2,1,0:T(2,128)S(1)}, f32[2,2,7168]{2,1,0:T(2,128)}, u32[]{:S(2)}) copy-start(f32[2,2,7168]{2,1,0:T(2,128)} %get-tuple-element.37) | copy-start | bytes 344068
  30.0 0.9 %copy-start.1 = (f32[2,2,7168]{2,1,0:T(2,128)S(1)}, f32[2,2,7168]{2,1,0:T(2,128)}, u32[]{:S(2)}) copy-start(f32[2,2,7168]{2,1,0:T(2,128)} %get-tuple-element.38) | copy-start | bytes 344068
  31.0 0.9 %copy-start = (f32[2,2,7168]{2,1,0:T(2,128)S(1)}, f32[2,2,7168]{2,1,0:T(2,128)}, u32[]{:S(2)}) copy-start(f32[2,2,7168]{2,1,0:T(2,128)} %get-tuple-element.39) | copy-start | bytes 344068

commit v2 on v1

--- a/solution.py
+++ b/solution.py
@@ -18,6 +18,8 @@
 bias_second = 1.0 - beta_second**step_count
 LANES = 128
 SUBLANES = 8
+VMEM_BYTES = 67043328
+ROOM = 8192
 
 
 def adam_update(master, moment, second, gradient):
@@ -41,30 +43,22 @@
     om_in,
     o1_in,
     o2_in,
-    out_w,
+    obuf,
     out_norm,
-    lm_out,
-    l1_out,
-    l2_out,
-    om_out,
-    o1_out,
-    o2_out,
+    lst,
+    ost,
     mine,
     other,
     sendbuf,
     recvbuf,
     wall,
     w32,
-    obuf,
-    lst,
-    ost,
     tsum,
     dsum,
     tpart,
     dpart,
     load_sem,
     state_sem,
-    store_sem,
     pair_s,
     pair_r,
     rs_s,
@@ -178,7 +172,7 @@
         cp.wait()
     w32[...] = jnp.zeros_like(w32)
     squares = jnp.zeros((pad, LANES), jnp.float32)
-    gather, own, stores = [], [], []
+    gather, own = [], []
     for c in range(chunks):
         cols = pl.ds(c * width, width)
         total = sendbuf[chip, :, cols].astype(jnp.float32)
@@ -229,13 +223,6 @@
         cp.start()
         own.append(cp)
 
-    for i, (ref, src) in enumerate(
-        zip((lm_out, l1_out, l2_out, om_out, o1_out, o2_out), [lst.at[i] for i in range(3)] + [ost.at[i] for i in range(3)])
-    ):
-        cp = pltpu.make_async_copy(src, ref, state_sem.at[i])
-        cp.start()
-        stores.append(cp)
-
     tpart[...] = squares
     tcopies = []
     for k in range(1, tensors):
@@ -278,16 +265,12 @@
             row.append(cp)
         forwards.append(row)
 
-    outs = []
     for c in range(chunks):
         cols = pl.ds(c * width, width)
         for cp in forwards[c]:
             cp.wait_recv()
         weights = wall[:, :, cols].reshape(n * pad, width)
         obuf[:, cols] = jnp.dot(back, weights, preferred_element_type=jnp.float32).astype(jnp.bfloat16)
-        cp = pltpu.make_async_copy(obuf.at[:, cols], out_w.at[:, cols], store_sem.at[c])
-        cp.start()
-        outs.append(cp)
 
     value = dpart[...]
     for k in range(1, n):
@@ -302,9 +285,18 @@
             gather[c][k - 1].wait_send()
         for cp in forwards[c]:
             cp.wait_send()
-    for cp in stores:
-        cp.wait()
-    for cp in outs:
+
+
+def store_kernel(weights, norm, new_local, new_offload, out_w, out_norm, *rest):
+    outs, sem = rest[:6], rest[6]
+    sources = [new_local.at[i] for i in range(3)] + [new_offload.at[i] for i in range(3)]
+    copies = []
+    for i, (src, dst) in enumerate(zip([weights] + sources, (out_w,) + outs)):
+        cp = pltpu.make_async_copy(src, dst, sem.at[i])
+        cp.start()
+        copies.append(cp)
+    out_norm[...] = norm[...]
+    for cp in copies:
         cp.wait()
 
 
@@ -317,16 +309,21 @@
     chips = n // 2
     used = local.shape[0] + offload.shape[0] * offload.shape[1]
     pad = -(-used // SUBLANES) * SUBLANES
+    kept_tile = -(-local.shape[0] // 4) * 4
+    held = columns * (2 * rows + 12 * (kept_tile + offload.shape[0] * offload.shape[1]))
+    limit = VMEM_BYTES - held - ROOM
     any_space = pl.BlockSpec(memory_space=pl.ANY)
+    hbm = pl.BlockSpec(memory_space=pltpu.HBM)
     smem = pl.BlockSpec(memory_space=pltpu.SMEM)
     dma = pltpu.SemaphoreType.DMA
     f32, bf16 = jnp.float32, jnp.bfloat16
-    outs = pl.pallas_call(
+    vmem = pl.BlockSpec(memory_space=pltpu.VMEM)
+    shapes = [((rows, columns), bf16), ((1, 1), f32), ((3,) + local.shape, f32), ((3,) + offload.shape, f32)]
+    weights, norm, new_local, new_offload = pl.pallas_call(
         functools.partial(kernel, n, tensors, chunks),
-        out_shape=[jax.ShapeDtypeStruct((rows, columns), bf16), jax.ShapeDtypeStruct((1, 1), f32)]
-        + [jax.ShapeDtypeStruct(s.shape, f32) for s in states],
-        in_specs=[smem, smem] + [any_space] * 7,
-        out_specs=[any_space, pl.BlockSpec(memory_space=pltpu.VMEM)] + [any_space] * 6,
+        out_shape=[pltpu.VMEM(*s) for s in shapes],
+        in_specs=[smem, smem] + [hbm] * 7,
+        out_specs=[vmem] * 4,
         scratch_shapes=[
             pltpu.VMEM((rows, columns), bf16),
             pltpu.VMEM((rows, columns), bf16),
@@ -334,16 +331,12 @@
             pltpu.VMEM((chips - 1, pad, columns), bf16),
             pltpu.VMEM((n, pad, columns), bf16),
             pltpu.VMEM((pad, columns), f32),
-            pltpu.VMEM((rows, columns), bf16),
-            pltpu.VMEM((3,) + local.shape, f32),
-            pltpu.VMEM((3,) + offload.shape, f32),
             pltpu.VMEM((tensors - 1, pad, LANES), f32),
             pltpu.VMEM((n - 1, pad, LANES), f32),
             pltpu.VMEM((pad, LANES), f32),
             pltpu.VMEM((pad, LANES), f32),
             dma,
             dma((6,)),
-            dma((chunks,)),
             dma((chunks,)),
             dma((chunks,)),
             dma((chips - 1, chunks)),
@@ -357,9 +350,21 @@
             dma((n - 1,)),
             dma((n - 1,)),
         ],
-        compiler_params=pltpu.CompilerParams(collective_id=0, has_side_effects=True),
+        compiler_params=pltpu.CompilerParams(
+            collective_id=0, has_side_effects=True, vmem_limit_bytes=limit
+        ),
         name="step",
     )(mask, owner, grads, *states)
+    outs = pl.pallas_call(
+        store_kernel,
+        out_shape=[jax.ShapeDtypeStruct((rows, columns), bf16), jax.ShapeDtypeStruct((1, 1), f32)]
+        + [jax.ShapeDtypeStruct(s.shape, f32) for s in states],
+        in_specs=[any_space, vmem, any_space, any_space],
+        out_specs=[any_space, vmem] + [any_space] * 6,
+        scratch_shapes=[dma((7,))],
+        compiler_params=pltpu.CompilerParams(vmem_limit_bytes=1 << 20),
+        name="store",
+    )(weights, norm, new_local, new_offload)
     return (outs[0], outs[1][0, 0]) + tuple(outs[2:])
 
 

time: 34 us -> 27 us (0.79)
  local copies, waits for them, and re-layouts: 7.28 us -> 0 us
  Pallas kernels: 24 us -> 26.1 us
  between operations: 2.44 us -> 0.64 us
    unnamed x19 -> x0, local copies, waits for them, and re-layouts: 7.28 us -> none
    pallas_call x0 -> x1, Pallas kernels: none -> 2.23 us  [body(): pl.pallas_call(store_kernel, out_shape=[jax.ShapeDtypeStruct((rows, colum...]
where the time goes in v2:
time: 27 us; the launch traced here: 26.8 us
  Pallas kernels  26.1 us (97%)
  between operations  0.64 us (2%)
    pallas_call x1, Pallas kernels, body(): pl.pallas_call(functools.partial(kernel, n, tensors, chunks), out_shape=[...  23.9 us
    pallas_call x1, Pallas kernels, body(): pl.pallas_call(store_kernel, out_shape=[jax.ShapeDtypeStruct((rows, colum...  2.23 us

profile of v2, /device:TPU:0, one launch (start us, length us, event | category | flops | bytes accessed | tf_op | source)
XLA Modules:
  0.0 26.8 jit_solution(7725623593404913755)
XLA Ops:
  0.6 23.9 %step.1 = (bf16[40,7168]{1,0:T(8,128)(2,1)S(1)}, f32[1,1]{1,0:T(1,128)}, f32[3,3,7168]{2,1,0:T(4,128)S(1)}, f32[3,2,2,7168]{3,2,1,0:T(2,128)S(1)}) custom-call(s32[8,5]{1,0:T(8,128)} %mask_ref.1, s32[8]{0:T(128)} %owner_ref.1, bf16[1,40,7168]{2,1,0:T(8,128)(2,1)} %grads.1, f32[3,7168]{1,0:T(4,128)} %lm_in.1, f32[3,7168]{1,0:T(4,128)} %l1_in.1, ...), custom_call_target="tpu_custom_call" | custom-call | tf_op jit(solution)/shard_map/step/pallas_call | solution.py:322
  24.5 2.2 %store.1 = (bf16[40,7168]{1,0:T(8,128)(2,1)}, f32[1,1]{1,0:T(1,128)}, f32[3,7168]{1,0:T(4,128)}, f32[3,7168]{1,0:T(4,128)}, f32[3,7168]{1,0:T(4,128)}, /*index=5...) custom-call(bf16[40,7168]{1,0:T(8,128)(2,1)S(1)} %get-tuple-element.20.weights, ...), custom_call_target="tpu_custom_call" | custom-call | tf_op jit(solution)/shard_map/store/pallas_call | solution.py:358

commit v3 on v2

--- a/solution.py
+++ b/solution.py
@@ -34,8 +34,8 @@
     n,
     tensors,
     chunks,
-    mask_ref,
-    owner_ref,
+    mask_in,
+    owner_in,
     grads,
     lm_in,
     l1_in,
@@ -47,6 +47,8 @@
     out_norm,
     lst,
     ost,
+    mask_ref,
+    owner_ref,
     mine,
     other,
     sendbuf,
@@ -59,6 +61,7 @@
     dpart,
     load_sem,
     state_sem,
+    table_sem,
     pair_s,
     pair_r,
     rs_s,
@@ -85,8 +88,23 @@
     width = columns // chunks
     pad = w32.shape[0]
 
+    barrier = pltpu.get_barrier_semaphore()
+
+    def greet(k, c):
+        pl.semaphore_signal(barrier, inc=1, device_id={"dp": lax.rem(dp + k, n)}, device_id_type=MESH)
+        return c
+
+    lax.fori_loop(1, n, greet, 0)
+    for k in range(1, tensors):
+        pl.semaphore_signal(barrier, inc=1, device_id={"tensor": lax.rem(tn + k, tensors)}, device_id_type=MESH)
+
     load = pltpu.make_async_copy(grads.at[0], mine, load_sem)
     load.start()
+    tables = []
+    for i, (ref, dst) in enumerate(((mask_in, mask_ref), (owner_in, owner_ref))):
+        cp = pltpu.make_async_copy(ref, dst, table_sem.at[i])
+        cp.start()
+        tables.append(cp)
     loads = []
     for i, (ref, dst) in enumerate(
         zip((lm_in, l1_in, l2_in, om_in, o1_in, o2_in), [lst.at[i] for i in range(3)] + [ost.at[i] for i in range(3)])
@@ -95,16 +113,8 @@
         cp.start()
         loads.append(cp)
 
-    barrier = pltpu.get_barrier_semaphore()
-
-    def greet(k, c):
-        pl.semaphore_signal(barrier, inc=1, device_id={"dp": lax.rem(dp + k, n)}, device_id_type=MESH)
-        return c
-
-    lax.fori_loop(1, n, greet, 0)
-    for k in range(1, tensors):
-        pl.semaphore_signal(barrier, inc=1, device_id={"tensor": lax.rem(tn + k, tensors)}, device_id_type=MESH)
-
+    for cp in tables:
+        cp.wait()
     lane = lax.broadcasted_iota(jnp.int32, (1, rows), 1)
     sub = lax.broadcasted_iota(jnp.int32, (rows, 1), 0)
 
@@ -231,24 +241,23 @@
         )
         cp.start()
         tcopies.append(cp)
-    for cp in tcopies:
-        cp.wait()
-
-    value = tpart[...]
-    for k in range(1, tensors):
-        value = value + tsum[k - 1]
-    dpart[...] = value
-    dcopies = []
-    for k in range(1, n):
-        cp = pltpu.make_async_remote_copy(
-            dpart, dsum.at[k - 1], d_s.at[k - 1], d_r.at[k - 1], device_id={"dp": lax.rem(dp + k, n)}, device_id_type=MESH
-        )
-        cp.start()
-        dcopies.append(cp)
-
     forwards = []
     for c in range(chunks):
         cols = pl.ds(c * width, width)
+        if c == chunks - 1:
+            for cp in tcopies:
+                cp.wait()
+            value = tpart[...]
+            for k in range(1, tensors):
+                value = value + tsum[k - 1]
+            dpart[...] = value
+            dcopies = []
+            for k in range(1, n):
+                cp = pltpu.make_async_remote_copy(
+                    dpart, dsum.at[k - 1], d_s.at[k - 1], d_r.at[k - 1], device_id={"dp": lax.rem(dp + k, n)}, device_id_type=MESH
+                )
+                cp.start()
+                dcopies.append(cp)
         row = [own[c]]
         for k in range(1, chips):
             gather[c][k - 1].wait_recv()
@@ -314,7 +323,6 @@
     limit = VMEM_BYTES - held - ROOM
     any_space = pl.BlockSpec(memory_space=pl.ANY)
     hbm = pl.BlockSpec(memory_space=pltpu.HBM)
-    smem = pl.BlockSpec(memory_space=pltpu.SMEM)
     dma = pltpu.SemaphoreType.DMA
     f32, bf16 = jnp.float32, jnp.bfloat16
     vmem = pl.BlockSpec(memory_space=pltpu.VMEM)
@@ -322,9 +330,11 @@
     weights, norm, new_local, new_offload = pl.pallas_call(
         functools.partial(kernel, n, tensors, chunks),
         out_shape=[pltpu.VMEM(*s) for s in shapes],
-        in_specs=[smem, smem] + [hbm] * 7,
+        in_specs=[hbm] * 9,
         out_specs=[vmem] * 4,
         scratch_shapes=[
+            pltpu.SMEM(mask.shape, jnp.int32),
+            pltpu.SMEM(owner.shape, jnp.int32),
             pltpu.VMEM((rows, columns), bf16),
             pltpu.VMEM((rows, columns), bf16),
             pltpu.VMEM((chips, pad, columns), bf16),
@@ -337,6 +347,7 @@
             pltpu.VMEM((pad, LANES), f32),
             dma,
             dma((6,)),
+            dma((2,)),
             dma((chunks,)),
             dma((chunks,)),
             dma((chips - 1, chunks)),

time: 27 us -> 26.2 us (0.970)
  Pallas kernels: 26.1 us -> 25.4 us
    pallas_call x1, Pallas kernels: 23.9 us -> 23.2 us  [body(): pl.pallas_call(functools.partial(kernel, n, tensors, chunks), out_shape=[...]
where the time goes in v3:
time: 26.2 us; the launch traced here: 26.1 us
  Pallas kernels  25.4 us (97%)
  between operations  0.64 us (2%)
    pallas_call x1, Pallas kernels, body(): pl.pallas_call(functools.partial(kernel, n, tensors, chunks), out_shape=[...  23.2 us
    pallas_call x1, Pallas kernels, body(): pl.pallas_call(store_kernel, out_shape=[jax.ShapeDtypeStruct((rows, colum...  2.23 us

profile of v3, /device:TPU:0, one launch (start us, length us, event | category | flops | bytes accessed | tf_op | source)
XLA Modules:
  0.0 26.1 jit_solution(16701768570663639140)
XLA Ops:
  0.6 23.2 %step.1 = (bf16[40,7168]{1,0:T(8,128)(2,1)S(1)}, f32[1,1]{1,0:T(1,128)}, f32[3,3,7168]{2,1,0:T(4,128)S(1)}, f32[3,2,2,7168]{3,2,1,0:T(2,128)S(1)}) custom-call(s32[8,5]{1,0:T(8,128)} %mask_in.1, s32[8]{0:T(128)} %owner_in.1, bf16[1,40,7168]{2,1,0:T(8,128)(2,1)} %grads.1, f32[3,7168]{1,0:T(4,128)} %lm_in.1, f32[3,7168]{1,0:T(4,128)} %l1_in.1, ...), custom_call_target="tpu_custom_call" | custom-call | tf_op jit(solution)/shard_map/step/pallas_call | solution.py:330
  23.8 2.2 %store.1 = (bf16[40,7168]{1,0:T(8,128)(2,1)}, f32[1,1]{1,0:T(1,128)}, f32[3,7168]{1,0:T(4,128)}, f32[3,7168]{1,0:T(4,128)}, f32[3,7168]{1,0:T(4,128)}, /*index=5...) custom-call(bf16[40,7168]{1,0:T(8,128)(2,1)S(1)} %get-tuple-element.20.weights, ...), custom_call_target="tpu_custom_call" | custom-call | tf_op jit(solution)/shard_map/store/pallas_call | solution.py:369

commit v4 on v3

--- a/solution.py
+++ b/solution.py
@@ -88,15 +88,20 @@
     width = columns // chunks
     pad = w32.shape[0]
 
+    def peer(k):
+        return sum((chip // b + k // b) % 2 * b for b in bits)
+
+    bits = [1 << i for i in range(chips.bit_length() - 1)]
+    order = sorted(range(1, chips), key=lambda k: -bin(k).count("1"))
     barrier = pltpu.get_barrier_semaphore()
 
     def greet(k, c):
         pl.semaphore_signal(barrier, inc=1, device_id={"dp": lax.rem(dp + k, n)}, device_id_type=MESH)
         return c
 
-    lax.fori_loop(1, n, greet, 0)
     for k in range(1, tensors):
         pl.semaphore_signal(barrier, inc=1, device_id={"tensor": lax.rem(tn + k, tensors)}, device_id_type=MESH)
+    lax.fori_loop(1, n, greet, 0)
 
     load = pltpu.make_async_copy(grads.at[0], mine, load_sem)
     load.start()
@@ -163,9 +168,9 @@
         both = mine[:, cols].astype(jnp.float32) + other[:, cols].astype(jnp.float32)
         routed = jnp.dot(route, both.astype(jnp.bfloat16), preferred_element_type=jnp.float32)
         sendbuf[:, :, cols] = routed.reshape(chips, pad, width).astype(jnp.bfloat16)
-        row = []
-        for k in range(1, chips):
-            to = lax.rem(chip + k, chips)
+        row = {}
+        for k in order:
+            to = peer(k)
             cp = pltpu.make_async_remote_copy(
                 sendbuf.at[to, :, cols],
                 recvbuf.at[k - 1, :, cols],
@@ -175,7 +180,7 @@
                 device_id_type=MESH,
             )
             cp.start()
-            row.append(cp)
+            row[k] = cp
         scatter.append(row)
 
     for cp in loads:
@@ -187,12 +192,21 @@
         cols = pl.ds(c * width, width)
         total = sendbuf[chip, :, cols].astype(jnp.float32)
         for k in range(1, chips):
-            scatter[c][k - 1].wait_recv()
+            scatter[c][k].wait_recv()
             total = total + recvbuf[k - 1, :, cols].astype(jnp.float32)
         total = total / n
         sq = total * total
         for v in range(width // LANES):
             squares = squares + sq[:, v * LANES : (v + 1) * LANES]
+        if c == chunks - 1:
+            tpart[...] = squares
+            tcopies = []
+            for k in range(1, tensors):
+                cp = pltpu.make_async_remote_copy(
+                    tpart, tsum.at[k - 1], t_s.at[k - 1], t_r.at[k - 1], device_id={"tensor": lax.rem(tn + k, tensors)}, device_id_type=MESH
+                )
+                cp.start()
+                tcopies.append(cp)
         new = adam_update(lst[0, :, cols], lst[1, :, cols], lst[2, :, cols], total[:kept])
         for i in range(3):
             lst[i, :, cols] = new[i]
@@ -208,9 +222,9 @@
                 if i == 0:
                     w32[first : first + off, cols] = value
         wall[dp, :, cols] = w32[:, cols].astype(jnp.bfloat16)
-        row = []
-        for k in range(1, chips):
-            to = lax.rem(chip + k, chips)
+        row = {}
+        for k in order:
+            to = peer(k)
             cp = pltpu.make_async_remote_copy(
                 wall.at[dp, :, cols],
                 wall.at[dp, :, cols],
@@ -220,7 +234,7 @@
                 device_id_type=MESH,
             )
             cp.start()
-            row.append(cp)
+            row[k] = cp
         gather.append(row)
         cp = pltpu.make_async_remote_copy(
             wall.at[dp, :, cols],
@@ -233,14 +247,6 @@
         cp.start()
         own.append(cp)
 
-    tpart[...] = squares
-    tcopies = []
-    for k in range(1, tensors):
-        cp = pltpu.make_async_remote_copy(
-            tpart, tsum.at[k - 1], t_s.at[k - 1], t_r.at[k - 1], device_id={"tensor": lax.rem(tn + k, tensors)}, device_id_type=MESH
-        )
-        cp.start()
-        tcopies.append(cp)
     forwards = []
     for c in range(chunks):
         cols = pl.ds(c * width, width)
@@ -260,8 +266,8 @@
                 dcopies.append(cp)
         row = [own[c]]
         for k in range(1, chips):
-            gather[c][k - 1].wait_recv()
-            src = lax.rem(chip + chips - k, chips) * 2 + core
+            gather[c][k].wait_recv()
+            src = peer(k) * 2 + core
             cp = pltpu.make_async_remote_copy(
                 wall.at[src, :, cols],
                 wall.at[src, :, cols],
@@ -290,8 +296,8 @@
     for c in range(chunks):
         pairs[c].wait_send()
         for k in range(1, chips):
-            scatter[c][k - 1].wait_send()
-            gather[c][k - 1].wait_send()
+            scatter[c][k].wait_send()
+            gather[c][k].wait_send()
         for cp in forwards[c]:
             cp.wait_send()
 
@@ -312,7 +318,7 @@
 def body(n, tensors, grads, mask, owner, *states):
     rows, columns = grads.shape[1:]
     local, offload = states[0], states[3]
-    chunks = 4
+    chunks = 2
     while columns % (chunks * LANES):
         chunks -= 1
     chips = n // 2

time: 26.2 us -> 25.2 us (0.962)
  Pallas kernels: 25.4 us -> 24.4 us
    pallas_call x1, Pallas kernels: 23.2 us -> 22.1 us  [body(): pl.pallas_call(functools.partial(kernel, n, tensors, chunks), out_shape=[...]
where the time goes in v4:
time: 25.2 us; the launch traced here: 25 us
  Pallas kernels  24.4 us (97%)
  between operations  0.64 us (3%)
    pallas_call x1, Pallas kernels, body(): pl.pallas_call(functools.partial(kernel, n, tensors, chunks), out_shape=[...  22.1 us
    pallas_call x1, Pallas kernels, body(): pl.pallas_call(store_kernel, out_shape=[jax.ShapeDtypeStruct((rows, colum...  2.23 us

profile of v4, /device:TPU:0, one launch (start us, length us, event | category | flops | bytes accessed | tf_op | source)
XLA Modules:
  0.0 25.0 jit_solution(5266956840947898715)
XLA Ops:
  0.6 22.1 %step.1 = (bf16[40,7168]{1,0:T(8,128)(2,1)S(1)}, f32[1,1]{1,0:T(1,128)}, f32[3,3,7168]{2,1,0:T(4,128)S(1)}, f32[3,2,2,7168]{3,2,1,0:T(2,128)S(1)}) custom-call(s32[8,5]{1,0:T(8,128)} %mask_in.1, s32[8]{0:T(128)} %owner_in.1, bf16[1,40,7168]{2,1,0:T(8,128)(2,1)} %grads.1, f32[3,7168]{1,0:T(4,128)} %lm_in.1, f32[3,7168]{1,0:T(4,128)} %l1_in.1, ...), custom_call_target="tpu_custom_call" | custom-call | tf_op jit(solution)/shard_map/step/pallas_call | solution.py:336
  22.8 2.2 %store.1 = (bf16[40,7168]{1,0:T(8,128)(2,1)}, f32[1,1]{1,0:T(1,128)}, f32[3,7168]{1,0:T(4,128)}, f32[3,7168]{1,0:T(4,128)}, f32[3,7168]{1,0:T(4,128)}, /*index=5...) custom-call(bf16[40,7168]{1,0:T(8,128)(2,1)S(1)} %get-tuple-element.20.weights, ...), custom_call_target="tpu_custom_call" | custom-call | tf_op jit(solution)/shard_map/store/pallas_call | solution.py:375
